TPU v7x, 32 devices: a whole 2x2x4 slice. The times are simulated.
32 devices in a mesh: dp: 8 (over z, x), fsdp: 4 (over y, core).
Axes of the slice: x: 2, y: 2, z: 4, core: 2. Of those that a mesh axis runs over, the one named last changes fastest.
Arguments:
- latents: bfloat16 [96, 2, 4096], P('dp'), may hold values from -6 to 6
- noise: bfloat16 [96, 2, 4096], P('dp'), may hold values from -6 to 6
- behavior_velocity: bfloat16 [96, 2, 4096], P('dp'), may hold values from -6 to 6
- timestep: int32 [96, 2], P('dp'), may hold values from 0 to 9
- reward_rank_integer: int32 [96], P('dp'), may hold values from 0 to 1023
- surviving_source_index: int32 [48], replicated, may hold values from 0 to 7, as said below
- surviving_slot_index: int32 [48], replicated, may hold values from 0 to 11, as said below
- group_kept_count: int32 [12], replicated, may hold values from 1 to 24, 48 in all
- patch_input_weight: bfloat16 [64, 1536], replicated, may hold values from -0.75 to 0.75
- modulation_lookup: float32 [10, 3, 1536], replicated, may hold values from -3 to 3
- up_projection_weight: bfloat16 [1536, 8192], P(None, 'fsdp'), may hold values from -0.15625 to 0.15625
- down_projection_weight: bfloat16 [1536, 8192], P(None, 'fsdp'), may hold values from -0.0625 to 0.0625
- velocity_head_weight: bfloat16 [1536, 64], replicated, may hold values from -0.15625 to 0.15625
Outputs:
- up_weight_gradient: float32 [1536, 8192], P('dp', 'fsdp')
- down_weight_gradient: float32 [1536, 8192], P('dp', 'fsdp')
- loss: float32 [], replicated
Inputs may be any that keep to these rules, and one draw needn't show every extreme that they name: `surviving_source_index`: survivors are listed by source in ascending order; survivor j is trained on dp index j // 6, and every survivor of source d is trained on dp index d or d + 1. `surviving_slot_index`: the slots of one source's survivors are distinct.
All inputs are finite; a program needn't handle non-finite values.
Results may differ from a plain program's by a relative error of at most 0.013.
Values may be sent and summed in bfloat16 or wider, within the bound.
A program may use at most 128 MiB of HBM per device.

v0:
```python
import jax
import jax.numpy as jnp
from jax import lax
from jax.sharding import PartitionSpec as P

KSTEPS = 10


clip_range = 0.2
noise_level = 0.7
norm_eps = 1e-06


def shortened(x):

    def short(part):
        return part.astype(jnp.bfloat16) if part.dtype == jnp.float32 else part

    return jax.tree.map(short, x)


def shifted(value, axis, steps):
    count = lax.axis_size(axis)
    initial, last = (max(0, -steps), min(count, count - steps))
    return lax.ppermute(value, axis, [(source, source + steps) for source in range(initial, last)])


def step_ratio(indices, count):
    spacing = 1.0 / count
    level = 1.0 - indices.astype(jnp.float32) * spacing
    return jnp.sqrt(spacing * (1.0 - level + spacing) / level) / noise_level


def layer_norm(values):
    center = values - jnp.mean(values, axis=-1, keepdims=True)
    variance = jnp.mean(center * center, axis=-1, keepdims=True)
    inverse = lax.rsqrt(variance + norm_eps)
    return (center * inverse, inverse)


def smooth_gate(values):
    return jax.nn.gelu(values, approximate=True)


def membership_matrix(surviving_identifiers, kept_mask):
    group_ends = jnp.cumsum(kept_mask)
    group_starts = group_ends - kept_mask
    inside_clip_mask = (surviving_identifiers[:, None] >= group_starts[None, :]) & (
        surviving_identifiers[:, None] < group_ends[None, :]
    )
    return inside_clip_mask.astype(jnp.int32)


def advantages(ranks, member_mask, kept_mask, sums):
    count = jnp.sum(member_mask * kept_mask[None, :], axis=1)
    first = jnp.sum(member_mask * sums[0][None, :], axis=1)
    second = jnp.sum(member_mask * sums[1][None, :], axis=1)
    spread = (count * second - first * first).astype(jnp.float32)
    counts = count.astype(jnp.float32)
    deviation = jnp.sqrt(spread) / counts
    return (ranks.astype(jnp.float32) - first.astype(jnp.float32) / counts) / jnp.maximum(
        deviation, 1.0
    )


def shards(
    latents,
    noise,
    behavior_velocity,
    timestep,
    reward_rank_integer,
    surviving_source_index,
    surviving_slot_index,
    group_kept_count,
    patch_input_weight,
    modulation_lookup,
    up_projection_weight,
    down_projection_weight,
    velocity_head_weight,
):
    owner = lax.axis_index("dp")
    owner_ranks = lax.axis_size("dp")
    surviving_count = surviving_source_index.shape[0]
    trajectory_rows = surviving_count // owner_ranks
    leading_identifier = owner * trajectory_rows
    owned_source_index = lax.dynamic_slice_in_dim(
        surviving_source_index, leading_identifier, trajectory_rows
    )
    owned_slot_index = lax.dynamic_slice_in_dim(
        surviving_slot_index, leading_identifier, trajectory_rows
    )
    local_data = (latents, noise, behavior_velocity, timestep, reward_rank_integer)

    def selection_mask(slot_list):
        return tuple((jnp.take(array, slot_list, axis=0) for array in local_data))

    own_rows = selection_mask(owned_slot_index)
    following_leader = jnp.minimum(owner + 1, owner_ranks - 1) * trajectory_rows
    outgoing_rows = selection_mask(
        lax.dynamic_slice_in_dim(surviving_slot_index, following_leader, trajectory_rows)
    )
    arrived = jax.tree.map(
        lambda part, own: part.astype(own.dtype),
        shifted(shortened(outgoing_rows), "dp", 1),
        outgoing_rows,
    )
    from_left = owned_source_index != owner
    gathered = tuple(
        (
            jnp.where(from_left.reshape((trajectory_rows,) + (1,) * (mine.ndim - 1)), came, mine)
            for mine, came in zip(own_rows, arrived)
        )
    )
    samples, noises, olds, stamps, ranks = gathered
    member_mask = membership_matrix(
        leading_identifier + jnp.arange(trajectory_rows, dtype=jnp.int32), group_kept_count
    )
    partial_value = jnp.stack(
        [
            jnp.sum(member_mask * ranks[:, None], axis=0),
            jnp.sum(member_mask * (ranks * ranks)[:, None], axis=0),
        ]
    ).astype(jnp.int32)
    totals = lax.psum(partial_value, "dp")
    advantage = advantages(ranks, member_mask, group_kept_count, totals)
    patch = patch_input_weight.shape[0]
    width = patch_input_weight.shape[1]
    hidden_shard = up_projection_weight.shape[1]
    step_indices = stamps.shape[1]
    units = trajectory_rows * step_indices
    seq = samples.shape[2] // patch
    rows = units * seq
    stamp_flat = stamps.reshape(units)
    modulation = jnp.take(modulation_lookup, stamp_flat, axis=0)
    embedded = jnp.dot(
        samples.reshape(rows, patch), patch_input_weight, preferred_element_type=jnp.float32
    ).reshape(units, seq, width)
    normed, unused_value = layer_norm(embedded)
    modulated = (
        (normed * (1.0 + modulation[:, 1][:, None]) + modulation[:, 0][:, None])
        .astype(jnp.bfloat16)
        .reshape(rows, width)
    )
    pre = jnp.dot(modulated, up_projection_weight, preferred_element_type=jnp.float32)
    activated = smooth_gate(pre).astype(jnp.bfloat16)
    projected = lax.dot_general(
        activated,
        down_projection_weight,
        (((1,), (1,)), ((), ())),
        preferred_element_type=jnp.float32,
    )
    per_unit_gain = jnp.repeat(advantage, step_indices)
    coeff = step_ratio(stamp_flat, KSTEPS)
    gates = modulation[:, 2]
    embedded_rows = embedded.reshape(rows, width)
    old_rows = olds.reshape(rows, patch)
    noise_rows = noises.reshape(rows, patch)

    def head_terms(summed, lower, count):
        row_ids = lower + jnp.arange(count, dtype=jnp.int32)
        owner_unit = row_ids // seq
        gate_rows = jnp.take(gates, owner_unit, axis=0)
        mixed = lax.dynamic_slice_in_dim(embedded_rows, lower, count) + gate_rows * summed
        final, inverse = layer_norm(mixed)
        velocity = jnp.dot(
            final.astype(jnp.bfloat16), velocity_head_weight, preferred_element_type=jnp.float32
        )
        target = lax.dynamic_slice_in_dim(old_rows, lower, count).astype(jnp.float32)
        drawn = lax.dynamic_slice_in_dim(noise_rows, lower, count).astype(jnp.float32)
        coeff_rows = jnp.take(coeff, owner_unit)[:, None]
        error = velocity - target
        terms = coeff_rows * drawn * error + 0.5 * coeff_rows * coeff_rows * error * error
        unit_member = (owner_unit[:, None] == jnp.arange(units, dtype=jnp.int32)[None, :]).astype(
            jnp.float32
        )
        unit_sums = jnp.sum(unit_member * jnp.sum(terms, axis=1)[:, None], axis=0)

        def backward(loss_slope):
            slope_rows = jnp.take(loss_slope, owner_unit)[:, None]
            dvelocity = (
                slope_rows
                * (-(coeff_rows * drawn + coeff_rows * coeff_rows * error) / (seq * patch))
            ).astype(jnp.bfloat16)
            dfinal = lax.dot_general(
                dvelocity,
                velocity_head_weight,
                (((1,), (1,)), ((), ())),
                preferred_element_type=jnp.float32,
            )
            dmixed = inverse * (
                dfinal
                - jnp.mean(dfinal, axis=-1, keepdims=True)
                - final * jnp.mean(dfinal * final, axis=-1, keepdims=True)
            )
            return (gate_rows * dmixed).astype(jnp.bfloat16)

        return (unit_sums, backward)

    share = rows // lax.axis_size("fsdp")
    lower = lax.axis_index("fsdp") * share
    summed = lax.psum_scatter(projected, "fsdp", scatter_dimension=0, tiled=True)
    part_sums, backward = head_terms(summed, lower, share)
    unit_sums = lax.psum(part_sums, "fsdp")
    logratio = -unit_sums / (seq * patch)
    likelihood_ratio = jnp.exp(logratio)
    clipped = jnp.clip(likelihood_ratio, 1.0 - clip_range, 1.0 + clip_range)
    plain = likelihood_ratio * per_unit_gain
    bounded = clipped * per_unit_gain
    unit_loss = -jnp.minimum(plain, bounded)
    live_mask = (plain <= bounded).astype(jnp.float32)
    loss_slope = -per_unit_gain * likelihood_ratio * live_mask / (surviving_count * step_indices)
    replica_loss, loss_slope = (jnp.sum(unit_loss), loss_slope)
    upstream = lax.all_gather(backward(loss_slope), "fsdp", axis=0, tiled=True)
    total_count = lax.psum(replica_loss, "dp") / (surviving_count * step_indices)
    dactivated = jnp.dot(upstream, down_projection_weight, preferred_element_type=jnp.float32)
    unused_value, pull = jax.vjp(smooth_gate, pre)
    dpre = pull(dactivated)[0].astype(jnp.bfloat16)
    contract = (((0,), (0,)), ((), ()))
    grads = lax.psum_scatter(
        jnp.concatenate(
            [
                lax.dot_general(modulated, dpre, contract, preferred_element_type=jnp.float32),
                lax.dot_general(upstream, activated, contract, preferred_element_type=jnp.float32),
            ],
            axis=1,
        ).astype(jnp.bfloat16),
        "dp",
        scatter_dimension=0,
        tiled=True,
    ).astype(jnp.float32)
    return (grads[:, :hidden_shard], grads[:, hidden_shard:], total_count)


def solution(mesh):
    return jax.shard_map(
        shards,
        mesh=mesh,
        in_specs=(
            P("dp", None, None),
            P("dp", None, None),
            P("dp", None, None),
            P("dp", None),
            P("dp"),
            P(),
            P(),
            P(),
            P(),
            P(),
            P(None, "fsdp"),
            P(None, "fsdp"),
            P(),
        ),
        out_specs=(P("dp", "fsdp"), P("dp", "fsdp"), P()),
        check_vma=False,
    )
```

profile of v0, /device:TPU:0, one launch (start us, length us, event | category | flops | bytes accessed | tf_op | source)
XLA Modules:
  0.0 407.1 jit_solution(13905212201470406815)
XLA Ops:
  7.2 0.9 compare_and_fusion.1
  8.1 1.3 gather_fusion.10
  9.4 4.9 %collective-permute-start.4 = (s32[6]{0:T(128)S(1)}, s32[6]{0:T(128)S(1)}, u32[]{:S(2)}, u32[]{:S(2)}) collective-permute-start(s32[6]{0:T(128)S(1)} %broadcast_select_fusion.11), channel_id=1, source_target_pairs={{0,4},{4,8},{8,12},{12,16},{16,20},{20,24},{24,28},{1,5},{5,9},{9,... | collective-permute-start | bytes 80 | tf_op jit(solution)/shard_map/ppermute | solution.py:25
  14.3 0.8 copy.22
  15.1 0.6 gather_fusion.4
  15.7 3.4 collective-permute-start.1
  19.2 1.7 gather_fusion.8
  20.8 1.7 gather_fusion.6
  22.5 1.7 gather_fusion.2
  24.2 0.3 broadcast_select_fusion.6
  24.5 3.4 collective-permute-start.3
  27.9 3.5 collective-permute-start.2
  31.4 3.4 collective-permute-start
  34.8 1.3 gather_fusion.11
  36.1 0.6 gather_fusion.5
  36.7 1.7 gather_fusion.9
  38.4 1.7 gather_fusion.7
  40.1 1.7 gather_fusion.3
  41.7 0.7 fusion.29
  42.6 0.1 reshape.239
  42.8 0.7 gather_fusion
  43.5 0.1 broadcast_select_fusion.9
  43.6 0.2 fusion.32
  43.9 0.5 broadcast_select_fusion
  44.3 0.2 reshape.238
  44.6 0.8 fusion.35
  45.4 0.6 multiply_reduce_fusion
  46.0 0.9 fusion.7
  46.9 0.8 copy-done.2
  47.8 1.4 copy-done.4
  49.2 0.7 slice-done.1
  49.9 5.0 %fusion.38 = f32[768,2048]{1,0:T(8,128)S(1)} fusion(bf16[768,1536]{1,0:T(8,128)(2,1)S(1)} %fusion.7, bf16[1536,2048]{1,0:T(8,128)(2,1)S(1)} %bitcast.70), kind=kOutput, calls=%fused_computation.149 | convolution fusion | flops 4831838208 | bytes 14942208 | tf_op jit(solution)/shard_map/dot_general | solution.py:144
  54.9 2.7 copy-done.9
  57.6 7.2 %fusion.26 = f32[768,1536]{1,0:T(8,128)} fusion(bf16[1536,2048]{1,0:T(8,128)(2,1)S(1)} %bitcast.72, f32[768,2048]{1,0:T(8,128)S(1)} %fusion.38), kind=kOutput, calls=%fused_computation.138 | convolution fusion | flops 4845993984 | bytes 17301504 | tf_op jit(solution)/shard_map/dot_general | solution.py:146
  64.9 0.6 copy-done.7
  65.4 0.2 reduce-window.8
  65.7 0.1 select_reduce_fusion.5
  65.8 8.8 %psum.22 = s32[2,12]{1,0:T(2,128)S(1)} all-reduce(s32[2,12]{1,0:T(2,128)S(1)} %pad_add_fusion), channel_id=1, replica_groups=mesh['dp'=8,'fsdp'=4] {'dp'}, use_global_device_ids=true, to_apply=%region_11.16 | all-reduce | flops 24 | bytes 192 | tf_op jit(solution)/shard_map/psum | solution.py:124
  74.6 0.2 select_reduce_fusion.1
  74.8 1.1 gather_fusion.1
  75.9 0.7 fusion.34
  76.6 7.6 %fusion.28 = (f32[192]{0:T(256)S(1)}, f32[192]{0:T(256)S(1)}) fusion(f32[]{:T(128)} %bitcast.15, f32[]{:T(128)} %bitcast.14, f32[]{:T(128)} %bitcast.13, f32[]{:T(128)} %bitcast.12, f32[]{:T(128)} %bitcast.11, f32[]{:T(128)} %bitcast.10, f32[]{:T(128)} %bitcast.9, f32[]{:T(128)} %bitcast.8, f32[]{:T(128)} %bitcast.7, f32[]{:T(128)} %bitcast.6, f32[]{:T(128)} %bitcast.5, ...), kind=kLoop, calls=%fused_computation.140 | loop fusion | flops 8832 | bytes 1588 | tf_op jit(solution)/shard_map/mul | solution.py:182
  84.2 0.2 reshape.242
  84.4 0.2 reshape.241
  84.7 0.1 copy.30
  84.8 0.1 copy.29
  84.8 26.4 %reduce-scatter.3.cloned.1.call-done = f32[192,1536]{1,0:T(8,128)} async-done(((f32[768,1536]{1,0:T(8,128)}), f32[192,1536]{1,0:T(8,128)}) %reduce-scatter.3.cloned.1.call-update) | async-done | bytes 1179664 | tf_op jit(solution)/shard_map/reduce_scatter | solution.py:201
  111.2 1.9 fusion.30
  113.2 0.3 multiply_reduce_fusion.2
  113.4 0.4 multiply_reduce_fusion.3
  113.8 0.1 select_reduce_fusion
  114.1 5.7 %psum.21 = f32[12]{0:T(128)S(1)} all-reduce(f32[12]{0:T(128)S(1)} %select_reduce_fusion), channel_id=1, replica_groups=mesh['dp'=8,'fsdp'=4] {'fsdp'}, use_global_device_ids=true, to_apply=%region_7.11 | all-reduce | flops 12 | bytes 96 | tf_op jit(solution)/shard_map/psum | solution.py:203
  119.9 0.6 minimum_reduce_fusion
  120.5 0.7 fusion.33
  121.1 7.5 %select_multiply_fusion = f32[192]{0:T(256)S(1)} fusion(f32[]{:T(128)} %bitcast.33, f32[]{:T(128)} %bitcast.32, f32[]{:T(128)} %bitcast.31, f32[]{:T(128)} %bitcast.30, f32[]{:T(128)} %bitcast.29, f32[]{:T(128)} %bitcast.28, f32[]{:T(128)} %bitcast.27, f32[]{:T(128)} %bitcast.26, f32[]{:T(128)} %bitcast.25, f32[]{:T(128)} %bitcast.24, f32[]{:T(128)} %bitcast.23, ...), kind=kLoop, calls=%fused_computation.97 | loop fusion | flops 8832 | bytes 820 | tf_op jit(solution)/shard_map/mul | solution.py:181
  128.6 0.5 fusion.27
  129.1 1.3 multiply_convert_fusion.1
  130.5 24.8 %all-gather.2.cloned.1.call-done = bf16[768,1536]{1,0:T(8,128)(2,1)} async-done(((bf16[192,1536]{1,0:T(8,128)(2,1)}), bf16[768,1536]{1,0:T(8,128)(2,1)}) %all-gather.2.cloned.1.call-update) | async-done | bytes 2359312 | tf_op jit(solution)/shard_map/all_gather | solution.py:213
  155.3 19.2 %convolution_convert_fusion.1 = bf16[1536,2048]{1,0:T(8,128)(2,1)} fusion(bf16[768,1536]{1,0:T(8,128)(2,1)} %copy-done.4, f32[768,2048]{1,0:T(8,128)} %copy-done.9, bf16[768,1536]{1,0:T(8,128)(2,1)} %all-gather.2.cloned.1.call-done, bf16[1536,2048]{1,0:T(8,128)(2,1)} %param.32), kind=kOutput, calls=%fused_computation.16 | convolution fusion | flops 9698279424 | bytes 23592960 | tf_op jit(solution)/shard_map/dot_general | solution.py:222
  174.5 8.7 %convolution_convert_fusion = bf16[1536,2048]{1,0:T(8,128)(2,1)S(1)} fusion(bf16[768,1536]{1,0:T(8,128)(2,1)S(1)} %copy-done.8, f32[768,2048]{1,0:T(8,128)} %copy-done.9), kind=kOutput, calls=%fused_computation.15 | convolution fusion | flops 4849139712 | bytes 14942208 | tf_op jit(solution)/shard_map/dot_general | solution.py:223
  183.2 5.1 %pad_maximum_fusion = bf16[1536,4096]{1,0:T(8,128)(2,1)} fusion(bf16[1536,2048]{1,0:T(8,128)(2,1)S(1)} %convolution_convert_fusion, bf16[1536,2048]{1,0:T(8,128)(2,1)S(1)} %copy-done.3), kind=kLoop, calls=%fused_computation.12 | loop fusion | flops 25165824 | bytes 25165824 | tf_op jit(solution)/shard_map/concatenate | solution.py:220
  189.0 22.6 %psum.23 = f32[]{:T(128)} all-reduce(f32[]{:T(128)S(6)} %neg.15), channel_id=1, replica_groups=mesh['dp'=8,'fsdp'=4] {'dp'}, use_global_device_ids=true, to_apply=%region_19.24 | all-reduce | flops 1 | bytes 8 | tf_op jit(solution)/shard_map/psum | solution.py:214
  212.2 183.8 %reduce-scatter.5.cloned.1.call-done = bf16[192,4096]{1,0:T(8,128)(2,1)} async-done(((bf16[1536,4096]{1,0:T(8,128)(2,1)}), bf16[192,4096]{1,0:T(8,128)(2,1)}) %reduce-scatter.5.cloned.1.call-update) | async-done | bytes 1572880 | tf_op jit(solution)/shard_map/reduce_scatter | solution.py:219
  396.0 3.4 fusion.31
  (67 shorter events, 0.8 us)
Async XLA Ops:
  7.2 35.6 %copy-start = (f32[10,3,1536]{2,1,0:T(4,128)S(1)}, f32[10,3,1536]{2,1,0:T(4,128)}, u32[]{:S(2)}) copy-start(f32[10,3,1536]{2,1,0:T(4,128)} %param.30) | copy-start | bytes 552964
  7.2 37.4 %copy-start.6 = (bf16[64,1536]{1,0:T(8,128)(2,1)S(1)}, bf16[64,1536]{1,0:T(8,128)(2,1)}, u32[]{:S(2)}) copy-start(bf16[64,1536]{1,0:T(8,128)(2,1)} %param.29) | copy-start | bytes 589828
  7.2 104.0 %reduce-scatter.3.cloned.1.call-start = ((), (), s32[]{:S(2)}) async-start(), calls=%async_computation.2 | async-start | bytes 5898240 | tf_op jit(solution)/shard_map/reduce_scatter | solution.py:201
  9.4 32.3 %collective-permute-start.4 = (s32[6]{0:T(128)S(1)}, s32[6]{0:T(128)S(1)}, u32[]{:S(2)}, u32[]{:S(2)}) collective-permute-start(s32[6]{0:T(128)S(1)} %broadcast_select_fusion.11), channel_id=1, source_target_pairs={{0,4},{4,8},{8,12},{12,16},{16,20},{20,24},{24,28},{1,5},{5,9},{9,... | collective-permute-start | bytes 80 | tf_op jit(solution)/shard_map/ppermute | solution.py:25
  15.7 26.8 %collective-permute-start.1 = (s32[6,2]{1,0:T(8,128)S(1)}, s32[6,2]{1,0:T(8,128)S(1)}, u32[]{:S(2)}, u32[]{:S(2)}) collective-permute-start(s32[6,2]{1,0:T(8,128)S(1)} %broadcast_select_fusion.10), channel_id=1, source_target_pairs={{0,4},{4,8},{8,12},{12,16},{16,20},{20,24},{24,28},{1,5},{5,9},{9,... | collective-permute-start | bytes 152 | tf_op jit(solution)/shard_map/ppermute | solution.py:25
  24.5 19.3 %collective-permute-start.3 = (bf16[6,2,4096]{2,1,0:T(2,128)(2,1)S(1)}, bf16[6,2,4096]{2,1,0:T(2,128)(2,1)S(1)}, u32[]{:S(2)}, u32[]{:S(2)}) collective-permute-start(bf16[6,2,4096]{2,1,0:T(2,128)(2,1)S(1)} %get-tuple-element.61), channel_id=1, source_target_pairs={{0,4},{4,8},{8,12},{12,16},{16,20},{20,24},{24,28},{1,5},{5,9},{9,... | collective-permute-start | bytes 294920 | tf_op jit(solution)/shard_map/ppermute | solution.py:25
  27.9 15.9 %collective-permute-start.2 = (bf16[6,2,4096]{2,1,0:T(2,128)(2,1)S(1)}, bf16[6,2,4096]{2,1,0:T(2,128)(2,1)S(1)}, u32[]{:S(2)}, u32[]{:S(2)}) collective-permute-start(bf16[6,2,4096]{2,1,0:T(2,128)(2,1)S(1)} %get-tuple-element.62), channel_id=1, source_target_pairs={{0,4},{4,8},{8,12},{12,16},{16,20},{20,24},{24,28},{1,5},{5,9},{9,... | collective-permute-start | bytes 294920 | tf_op jit(solution)/shard_map/ppermute | solution.py:25
  31.4 12.4 %collective-permute-start = (bf16[6,2,4096]{2,1,0:T(2,128)(2,1)S(1)}, bf16[6,2,4096]{2,1,0:T(2,128)(2,1)S(1)}, u32[]{:S(2)}, u32[]{:S(2)}) collective-permute-start(bf16[6,2,4096]{2,1,0:T(2,128)(2,1)S(1)} %get-tuple-element.63), channel_id=1, source_target_pairs={{0,4},{4,8},{8,12},{12,16},{16,20},{20,24},{24,28},{1,5},{5,9},{9,... | collective-permute-start | bytes 294920 | tf_op jit(solution)/shard_map/ppermute | solution.py:25
  44.5 4.6 %slice-start = ((s8[6291456]{0:T(1024)(128)(4,1)}), s8[4194304]{0:T(1024)(128)(4,1)S(1)}, s32[]{:S(2)}) async-start(s8[6291456]{0:T(1024)(128)(4,1)} %bitcast.69), calls=%async_computation.5 | async-start | bytes 8388608
  45.4 2.4 copy-start.2
  45.4 4.5 %slice-start.1 = ((s8[6291456]{0:T(1024)(128)(4,1)}), s8[2097152]{0:T(1024)(128)(4,1)S(1)}, s32[]{:S(2)}) async-start(s8[6291456]{0:T(1024)(128)(4,1)} %bitcast.69), calls=%async_computation.6 | async-start | bytes 4194304
  46.0 11.6 %slice-start.2 = ((s8[6291456]{0:T(1024)(128)(4,1)}), s8[4194304]{0:T(1024)(128)(4,1)S(1)}, s32[]{:S(2)}) async-start(s8[6291456]{0:T(1024)(128)(4,1)} %bitcast.71), calls=%async_computation.7 | async-start | bytes 8388608
  47.8 1.4 copy-start.4
  49.9 7.7 %slice-start.3 = ((s8[6291456]{0:T(1024)(128)(4,1)}), s8[2097152]{0:T(1024)(128)(4,1)S(1)}, s32[]{:S(2)}) async-start(s8[6291456]{0:T(1024)(128)(4,1)} %bitcast.71), calls=%async_computation.8 | async-start | bytes 4194304
  54.9 2.7 copy-start.9
  64.8 0.7 copy-start.7
  64.8 90.5 %all-gather.2.cloned.1.call-start = ((), (), s32[]{:S(2)}) async-start(), calls=%async_computation.3 | async-start | bytes 2949120 | tf_op jit(solution)/shard_map/all_gather | solution.py:213
  75.9 37.6 %copy-start.5 = (bf16[1536,64]{0,1:T(8,128)(2,1)S(1)}, bf16[1536,64]{0,1:T(8,128)(2,1)}, u32[]{:S(2)}) copy-start(bf16[1536,64]{0,1:T(8,128)(2,1)} %param.33) | copy-start | bytes 589828
  130.5 265.6 %reduce-scatter.5.cloned.1.call-start = ((), (), s32[]{:S(2)}) async-start(), calls=%async_computation.4 | async-start | bytes 14155776 | tf_op jit(solution)/shard_map/reduce_scatter | solution.py:219
  155.3 19.2 %copy-start.8 = (bf16[768,1536]{1,0:T(8,128)(2,1)S(1)}, bf16[768,1536]{1,0:T(8,128)(2,1)}, u32[]{:S(2)}) copy-start(bf16[768,1536]{1,0:T(8,128)(2,1)} %all-gather.2.cloned.1.call-done) | copy-start | bytes 7077892
  174.5 8.7 %copy-start.3 = (bf16[1536,2048]{1,0:T(8,128)(2,1)S(1)}, bf16[1536,2048]{1,0:T(8,128)(2,1)}, u32[]{:S(2)}) copy-start(bf16[1536,2048]{1,0:T(8,128)(2,1)} %convolution_convert_fusion.1) | copy-start | bytes 18874372
  188.3 211.1 %copy-start.1 = (f32[10,3,1536]{2,1,0:T(4,128)S(1)}, f32[10,3,1536]{2,1,0:T(4,128)}, u32[]{:S(2)}) copy-start(f32[10,3,1536]{2,1,0:T(4,128)} %param.30) | copy-start | bytes 552964
Sparse Core Ops, SparseCore 0:
  64.9 46.2 reduce-scatter.2
  130.6 24.6 all-gather.1
  188.5 207.5 reduce-scatter.4
where the time goes:
time: 408 us; the launch traced here: 407 us
  waiting for transfers between devices  235 us (58%)
  matrix products  41.9 us (10%)
  blocking collectives  37.1 us (9%)
  other arithmetic  29.4 us (7%)
  local copies, waits for them, and re-layouts  28.4 us (7%)
  starting transfers between devices  18.7 us (5%)
  between operations  16.7 us (4%)
    reduce_scatter x1, waiting for transfers between devices, shards(): lax.psum_scatter(jnp.concatenate([lax.dot_general(modulated, dpre, contra...  184 us
    reduce_scatter x1, waiting for transfers between devices, shards(): lax.psum_scatter(projected, 'fsdp', scatter_dimension=0, tiled=True)  26.4 us
    all_gather x1, waiting for transfers between devices, shards(): upstream = lax.all_gather(backward(loss_slope), 'fsdp', axis=0, tiled=True)  24.8 us
    psum x1, blocking collectives, shards(): lax.psum(replica_loss, 'dp') / (surviving_count * step_indices)  22.6 us
    dot_general x1, matrix products, shards(): lax.dot_general(modulated, dpre, contract, preferred_element_type=jnp.flo...  19.2 us
    ppermute x5, starting transfers between devices, shifted(): lax.ppermute(value, axis, [(source, source + steps) for source in range(i...  18.6 us
    gather x10, local copies, waits for them, and re-layouts, selection_mask(): return tuple((jnp.take(array, slot_list, axis=0) for array in local_data))  13.7 us
    psum x1, blocking collectives, shards(): totals = lax.psum(partial_value, 'dp')  8.76 us
  transfers between devices with their start and end apart: 8, of which 3 were waited for; matrix products, arithmetic and copies ran while one was open for 6% of the time, Pallas kernels for 0%

commit v1 on v0

--- a/solution.py
+++ b/solution.py
@@ -1,6 +1,10 @@
+import functools
+
 import jax
 import jax.numpy as jnp
 from jax import lax
+from jax.experimental import pallas as pl
+from jax.experimental.pallas import tpu as pltpu
 from jax.sharding import PartitionSpec as P
 
 KSTEPS = 10
@@ -61,6 +65,114 @@
     return (ranks.astype(jnp.float32) - first.astype(jnp.float32) / counts) / jnp.maximum(
         deviation, 1.0
     )
+
+
+def ring_place(index, count):
+    odd = index % 2
+    return (1 - odd) * (index // 2) + odd * (count - 1 - index // 2)
+
+
+def ring_index(place, count):
+    back = place // (count // 2)
+    return (1 - back) * (2 * place) + back * (2 * (count - 1 - place) + 1)
+
+
+def gradient_ring(
+    count, pieces, modulated, dpre, upstream, activated, up_out, down_out, sent, came, send_sem, recv_sem
+):
+    index = lax.axis_index("dp")
+    place = ring_place(index, count)
+    following = ring_index((place + 1) % count, count)
+    preceding = ring_index((place + count - 1) % count, count)
+    barrier = pltpu.get_barrier_semaphore()
+    for neighbour in (following, preceding):
+        pl.semaphore_signal(
+            barrier, inc=1, device_id={"dp": neighbour}, device_id_type=pl.DeviceIdType.MESH
+        )
+    pl.semaphore_wait(barrier, 2)
+    block = modulated.shape[0] // count
+    span = dpre.shape[1] // pieces
+    factors = ((modulated, dpre), (upstream, activated))
+    partners = (following, preceding)
+    outs = (up_out, down_out)
+
+    def target(way, step):
+        turn = (place + 2 * count - 1 - step) if way == 0 else (place + 1 + step)
+        return ring_index(turn % count, count)
+
+    def own(way, step, piece):
+        left, right = factors[way]
+        rows = pl.ds(pl.multiple_of(target(way, step) * block, block), block)
+        return jnp.dot(
+            left[rows, :],
+            right[:, piece * span : (piece + 1) * span],
+            preferred_element_type=jnp.float32,
+        )
+
+    def copy(way, step, piece):
+        return pltpu.make_async_remote_copy(
+            src_ref=sent.at[way, piece, step],
+            dst_ref=came.at[way, piece, step],
+            send_sem=send_sem.at[way, piece, step],
+            recv_sem=recv_sem.at[way, piece, step],
+            device_id={"dp": partners[way]},
+            device_id_type=pl.DeviceIdType.MESH,
+        )
+
+    order = [(way, piece) for piece in range(pieces) for way in range(2)]
+    for way, piece in order:
+        sent[way, piece, 0] = own(way, 0, piece).astype(jnp.bfloat16)
+        copy(way, 0, piece).start()
+
+    def hop(step, carry):
+        for way, piece in order:
+            part = own(way, step, piece)
+            copy(way, step - 1, piece).wait_recv()
+            sent[way, piece, step] = (
+                part + came[way, piece, step - 1].astype(jnp.float32)
+            ).astype(jnp.bfloat16)
+            copy(way, step, piece).start()
+        return carry
+
+    lax.fori_loop(1, count - 1, hop, 0)
+    for way, piece in order:
+        part = own(way, count - 1, piece)
+        copy(way, count - 2, piece).wait_recv()
+        outs[way][:, piece * span : (piece + 1) * span] = part + came[
+            way, piece, count - 2
+        ].astype(jnp.float32)
+
+    def drain(step, carry):
+        for way, piece in order:
+            copy(way, step, piece).wait_send()
+        return carry
+
+    lax.fori_loop(0, count - 1, drain, 0)
+
+
+def reduced_gradients(modulated, dpre, upstream, activated):
+    count = lax.axis_size("dp")
+    pieces = max(1, 32 // count)
+    block = modulated.shape[0] // count
+    span = dpre.shape[1] // pieces
+    shape = jax.ShapeDtypeStruct((block, dpre.shape[1]), jnp.float32)
+    hops = (2, pieces, count - 1)
+    return pl.pallas_call(
+        functools.partial(gradient_ring, count, pieces),
+        out_shape=(shape, shape),
+        in_specs=[pl.BlockSpec(memory_space=pltpu.VMEM)] * 4,
+        out_specs=(pl.BlockSpec(memory_space=pltpu.VMEM),) * 2,
+        scratch_shapes=[
+            pltpu.VMEM(hops + (block, span), jnp.bfloat16),
+            pltpu.VMEM(hops + (block, span), jnp.bfloat16),
+            pltpu.SemaphoreType.DMA(hops),
+            pltpu.SemaphoreType.DMA(hops),
+        ],
+        compiler_params=pltpu.CompilerParams(
+            collective_id=0, has_side_effects=True, vmem_limit_bytes=56 * 1024 * 1024
+        ),
+        name="gradient_ring",
+    )(modulated, dpre, upstream, activated)
 
 
 def shards(
@@ -89,46 +201,67 @@
     owned_slot_index = lax.dynamic_slice_in_dim(
         surviving_slot_index, leading_identifier, trajectory_rows
     )
-    local_data = (latents, noise, behavior_velocity, timestep, reward_rank_integer)
-
-    def selection_mask(slot_list):
-        return tuple((jnp.take(array, slot_list, axis=0) for array in local_data))
-
-    own_rows = selection_mask(owned_slot_index)
+    slots, step_indices, values = latents.shape
+    slot_ids = jnp.arange(slots, dtype=jnp.int32)
     following_leader = jnp.minimum(owner + 1, owner_ranks - 1) * trajectory_rows
-    outgoing_rows = selection_mask(
-        lax.dynamic_slice_in_dim(surviving_slot_index, following_leader, trajectory_rows)
-    )
-    arrived = jax.tree.map(
-        lambda part, own: part.astype(own.dtype),
-        shifted(shortened(outgoing_rows), "dp", 1),
-        outgoing_rows,
-    )
-    from_left = owned_source_index != owner
-    gathered = tuple(
-        (
-            jnp.where(from_left.reshape((trajectory_rows,) + (1,) * (mine.ndim - 1)), came, mine)
-            for mine, came in zip(own_rows, arrived)
-        )
-    )
-    samples, noises, olds, stamps, ranks = gathered
-    member_mask = membership_matrix(
-        leading_identifier + jnp.arange(trajectory_rows, dtype=jnp.int32), group_kept_count
+    outgoing_slot_index = lax.dynamic_slice_in_dim(
+        surviving_slot_index, following_leader, trajectory_rows
+    )
+    picks = jnp.concatenate([owned_slot_index, outgoing_slot_index])
+    chosen = picks[:, None] == slot_ids[None, :]
+    whole_numbers = jnp.concatenate(
+        [timestep, reward_rank_integer[:, None] // 32, reward_rank_integer[:, None] % 32], axis=1
+    )
+    numbers = jnp.sum(jnp.where(chosen[:, :, None], whole_numbers[None], 0), axis=1)
+    select = chosen.astype(jnp.bfloat16)
+    wide = step_indices * values
+
+    def picked(array):
+        return jnp.dot(
+            select, array.reshape(slots, wide), preferred_element_type=jnp.float32
+        ).astype(jnp.bfloat16)
+
+    packed = jnp.concatenate(
+        [
+            picked(latents),
+            picked(noise),
+            picked(behavior_velocity),
+            jnp.pad(numbers, ((0, 0), (0, 128 - numbers.shape[1]))).astype(jnp.bfloat16),
+        ],
+        axis=1,
+    )
+    arrived = shifted(packed[trajectory_rows:], "dp", 1)
+    member_all = membership_matrix(jnp.arange(surviving_count, dtype=jnp.int32), group_kept_count)
+    here = (surviving_source_index == owner).astype(jnp.int32)
+    survivor_ranks = here * jnp.sum(
+        jnp.where(
+            surviving_slot_index[:, None] == slot_ids[None, :], reward_rank_integer[None, :], 0
+        ),
+        axis=1,
     )
     partial_value = jnp.stack(
         [
-            jnp.sum(member_mask * ranks[:, None], axis=0),
-            jnp.sum(member_mask * (ranks * ranks)[:, None], axis=0),
+            jnp.sum(member_all * survivor_ranks[:, None], axis=0),
+            jnp.sum(member_all * (survivor_ranks * survivor_ranks)[:, None], axis=0),
         ]
     ).astype(jnp.int32)
     totals = lax.psum(partial_value, "dp")
+    from_left = owned_source_index != owner
+    gathered = jnp.where(from_left[:, None], arrived, packed[:trajectory_rows])
+    samples = gathered[:, :wide]
+    noises = gathered[:, wide : 2 * wide]
+    olds = gathered[:, 2 * wide : 3 * wide]
+    integers = gathered[:, 3 * wide :].astype(jnp.int32)
+    stamps = integers[:, :step_indices]
+    ranks = integers[:, step_indices] * 32 + integers[:, step_indices + 1]
+    member_mask = membership_matrix(
+        leading_identifier + jnp.arange(trajectory_rows, dtype=jnp.int32), group_kept_count
+    )
     advantage = advantages(ranks, member_mask, group_kept_count, totals)
     patch = patch_input_weight.shape[0]
     width = patch_input_weight.shape[1]
-    hidden_shard = up_projection_weight.shape[1]
-    step_indices = stamps.shape[1]
     units = trajectory_rows * step_indices
-    seq = samples.shape[2] // patch
+    seq = values // patch
     rows = units * seq
     stamp_flat = stamps.reshape(units)
     modulation = jnp.take(modulation_lookup, stamp_flat, axis=0)
@@ -148,7 +281,7 @@
         down_projection_weight,
         (((1,), (1,)), ((), ())),
         preferred_element_type=jnp.float32,
-    )
+    ).astype(jnp.bfloat16)
     per_unit_gain = jnp.repeat(advantage, step_indices)
     coeff = step_ratio(stamp_flat, KSTEPS)
     gates = modulation[:, 2]
@@ -198,9 +331,12 @@
 
     share = rows // lax.axis_size("fsdp")
     lower = lax.axis_index("fsdp") * share
-    summed = lax.psum_scatter(projected, "fsdp", scatter_dimension=0, tiled=True)
+    summed = lax.psum_scatter(
+        projected, "fsdp", scatter_dimension=0, tiled=True
+    ).astype(jnp.float32)
     part_sums, backward = head_terms(summed, lower, share)
-    unit_sums = lax.psum(part_sums, "fsdp")
+    whole_units = share % seq == 0
+    unit_sums = part_sums if whole_units else lax.psum(part_sums, "fsdp")
     logratio = -unit_sums / (seq * patch)
     likelihood_ratio = jnp.exp(logratio)
     clipped = jnp.clip(likelihood_ratio, 1.0 - clip_range, 1.0 + clip_range)
@@ -209,26 +345,19 @@
     unit_loss = -jnp.minimum(plain, bounded)
     live_mask = (plain <= bounded).astype(jnp.float32)
     loss_slope = -per_unit_gain * likelihood_ratio * live_mask / (surviving_count * step_indices)
-    replica_loss, loss_slope = (jnp.sum(unit_loss), loss_slope)
+    if whole_units:
+        unit_ids = jnp.arange(units, dtype=jnp.int32)
+        mine = (unit_ids >= lower // seq) & (unit_ids < (lower + share) // seq)
+        total_count = lax.psum(jnp.sum(jnp.where(mine, unit_loss, 0.0)), ("dp", "fsdp"))
+    else:
+        total_count = lax.psum(jnp.sum(unit_loss), "dp")
+    total_count = total_count / (surviving_count * step_indices)
     upstream = lax.all_gather(backward(loss_slope), "fsdp", axis=0, tiled=True)
-    total_count = lax.psum(replica_loss, "dp") / (surviving_count * step_indices)
     dactivated = jnp.dot(upstream, down_projection_weight, preferred_element_type=jnp.float32)
     unused_value, pull = jax.vjp(smooth_gate, pre)
     dpre = pull(dactivated)[0].astype(jnp.bfloat16)
-    contract = (((0,), (0,)), ((), ()))
-    grads = lax.psum_scatter(
-        jnp.concatenate(
-            [
-                lax.dot_general(modulated, dpre, contract, preferred_element_type=jnp.float32),
-                lax.dot_general(upstream, activated, contract, preferred_element_type=jnp.float32),
-            ],
-            axis=1,
-        ).astype(jnp.bfloat16),
-        "dp",
-        scatter_dimension=0,
-        tiled=True,
-    ).astype(jnp.float32)
-    return (grads[:, :hidden_shard], grads[:, hidden_shard:], total_count)
+    up_gradient, down_gradient = reduced_gradients(modulated.T, dpre, upstream.T, activated)
+    return (up_gradient, down_gradient, total_count)
 
 
 def solution(mesh):

time: 408 us -> 333 us (0.82)
  waiting for transfers between devices: 235 us -> 18.3 us
  Pallas kernels: 0 us -> 130 us
  blocking collectives: 37.1 us -> 53.4 us
  local copies, waits for them, and re-layouts: 28.4 us -> 42.9 us
  starting transfers between devices: 18.7 us -> 5.16 us
  matrix products: 41.9 us -> 35.5 us
    reduce_scatter x1 -> x0, waiting for transfers between devices: 184 us -> none  [shards(): lax.psum_scatter(jnp.concatenate([lax.dot_general(modulated, dpre, contra...]
    pallas_call x0 -> x1, Pallas kernels: none -> 130 us  [reduced_gradients(): pl.pallas_call(functools.partial(gradient_ring, count, pieces), out_shape...]
    all_gather x1, waiting for transfers between devices: 24.8 us -> 0.02 us  [shards(): upstream = lax.all_gather(backward(loss_slope), 'fsdp', axis=0, tiled=True)]
    reduce_scatter x1, waiting for transfers between devices: 26.4 us -> 10.2 us  [shards(): lax.psum_scatter(projected, 'fsdp', scatter_dimension=0, tiled=True)]
    dot_general x2 -> x4, matrix products: 27.9 us -> 13.9 us  [the longest x1 13 us: shards(): jnp.dot(upstream, down_projection_weight, preferred_element_type=jnp.floa...]
    gather x10 -> x0, local copies, waits for them, and re-layouts: 13.7 us -> none  [selection_mask(): return tuple((jnp.take(array, slot_list, axis=0) for array in local_data))]
    ppermute x5 -> x1, starting transfers between devices: 18.6 us -> 5.08 us  [shifted(): lax.ppermute(value, axis, [(source, source + steps) for source in range(i...]
    psum x2 -> x1, blocking collectives: 28.3 us -> 39.9 us  [shards(): lax.psum(jnp.sum(jnp.where(mine, unit_loss, 0.0)), ('dp', 'fsdp'))]
  transfers between devices with their start and end apart: 8 -> 3, of which waited for: 3 -> 2; matrix products, arithmetic and copies ran while one was open for 6% -> 3% of each run, Pallas kernels for 0% -> 0%
where the time goes in v1:
time: 333 us; the launch traced here: 332 us
  Pallas kernels  130 us (39%)
  blocking collectives  53.4 us (16%)
  local copies, waits for them, and re-layouts  42.9 us (13%)
  matrix products  35.5 us (11%)
  other arithmetic  31.2 us (9%)
  waiting for transfers between devices  18.3 us (5%)
  between operations  16.3 us (5%)
  starting transfers between devices  5.16 us (2%)
    pallas_call x1, Pallas kernels, reduced_gradients(): pl.pallas_call(functools.partial(gradient_ring, count, pieces), out_shape...  130 us
    psum x1, blocking collectives, shards(): lax.psum(jnp.sum(jnp.where(mine, unit_loss, 0.0)), ('dp', 'fsdp'))  39.9 us
    psum x1, blocking collectives, shards(): totals = lax.psum(partial_value, 'dp')  13.5 us
    dot_general x1, matrix products, shards(): jnp.dot(upstream, down_projection_weight, preferred_element_type=jnp.floa...  13 us
    reduce_scatter x1, waiting for transfers between devices, shards(): lax.psum_scatter(projected, 'fsdp', scatter_dimension=0, tiled=True)  10.2 us
    unnamed x44, local copies, waits for them, and re-layouts  9.64 us
    dot_general x1, matrix products, shards(): lax.dot_general(activated, down_projection_weight, (((1,), (1,)), ((), ()...  9.17 us
    mul x2, local copies, waits for them, and re-layouts, shards(): normed * (1.0 + modulation[:, 1][:, None]) + modulation[:, 0][:, None]  8.83 us
  transfers between devices with their start and end apart: 3, of which 2 were waited for; matrix products, arithmetic and copies ran while one was open for 3% of the time, Pallas kernels for 0%

profile of v1, /device:TPU:0, one launch (start us, length us, event | category | flops | bytes accessed | tf_op | source)
XLA Modules:
  0.0 332.4 jit_solution(17039322417434298771)
XLA Ops:
  7.2 0.7 fusion.27
  8.0 0.8 fusion.36
  8.9 0.7 pad_add_fusion
  9.6 0.3 select_reduce_fusion
  9.9 1.1 pad.22
  11.1 0.2 copy.64
  11.2 0.3 convolution_convert_fusion
  11.5 1.1 pad.21
  12.7 0.2 copy.63
  12.8 0.3 convolution_convert_fusion.1
  13.1 0.2 pad.20
  13.3 0.2 copy.62
  13.5 0.3 convolution_convert_fusion.2
  13.8 0.1 slice.110
  13.9 5.1 %collective-permute-start = (bf16[6,24704]{1,0:T(8,128)(2,1)S(1)}, bf16[6,24704]{1,0:T(8,128)(2,1)S(1)}, u32[]{:S(2)}, u32[]{:S(2)}) collective-permute-start(bf16[6,24704]{1,0:T(8,128)(2,1)S(1)} %slice.110), channel_id=1, source_target_pairs={{0,4},{4,8},{8,12},{12,16},{16,20},{20,24},{24,28},{1,5},{5,9},{9,... | collective-permute-start | bytes 889352 | tf_op jit(solution)/shard_map/ppermute | solution.py:29
  19.0 0.1 dynamic-slice_compare_fusion
  19.1 8.1 %collective-permute-done = bf16[6,24704]{1,0:T(8,128)(2,1)S(1)} collective-permute-done((bf16[6,24704]{1,0:T(8,128)(2,1)S(1)}, bf16[6,24704]{1,0:T(8,128)(2,1)S(1)}, u32[]{:S(2)}, u32[]{:S(2)}) %collective-permute-start) | collective-permute-done | bytes 296480 | tf_op jit(solution)/shard_map/ppermute | solution.py:29
  27.2 0.1 slice_select_fusion
  27.6 0.7 gather_fusion
  28.3 0.1 broadcast_select_fusion
  28.5 0.2 fusion.33
  28.7 2.8 add.210
  31.4 6.0 %copy.49 = f32[768,1536]{0,1:T(8,128)} copy(f32[768,1536]{1,0:T(8,128)} %bitcast.76) | data formatting | bytes 9437184 | tf_op jit(solution)/shard_map/add | solution.py:273
  37.5 2.8 mul.277
  40.2 6.1 %copy.48 = f32[768,1536]{0,1:T(8,128)} copy(f32[768,1536]{1,0:T(8,128)} %bitcast.77) | data formatting | bytes 9437184 | tf_op jit(solution)/shard_map/mul | solution.py:273
  46.3 0.2 reshape.301
  46.5 3.0 fusion.37
  49.5 6.1 %copy.47 = f32[768,1536]{0,1:T(8,128)} copy(f32[768,1536]{1,0:T(8,128)} %get-tuple-element.60) | data formatting | bytes 9437184 | tf_op jit(solution)/shard_map/dot_general | solution.py:268
  55.5 3.0 multiply_reduce_fusion
  58.6 0.7 copy-done.2
  59.3 5.4 %add_convert_fusion = bf16[768,1536]{0,1:T(8,128)(2,1)S(1)} fusion(f32[768,1536]{0,1:T(8,128)} %copy.49, f32[768,1536]{0,1:T(8,128)} %copy.48, f32[768,1536]{0,1:T(8,128)S(1)} %copy-done.2, f32[768]{0:T(1024)S(1)} %add_rsqrt_fusion, f32[768]{0:T(1024)S(1)} %broadcast_multiply_fusion), kind=kLoop, calls=%fused_computation.15 | loop fusion | flops 5898240 | bytes 16521216 | tf_op jit(solution)/shard_map/convert_element_type | solution.py:274
  64.7 8.5 %multiply_convert_fusion = (bf16[768,2048]{1,0:T(8,128)(2,1)S(1)}, f32[768,2048]{1,0:T(8,128)}) fusion(bf16[768,1536]{0,1:T(8,128)(2,1)S(1)} %add_convert_fusion, bf16[1536,2048]{1,0:T(8,128)(2,1)S(1)} %bitcast.95), kind=kOutput, calls=%fused_computation.14 | convolution fusion | flops 4845993984 | bytes 18087936 | tf_op jit(solution)/shard_map/dot_general | solution.py:277
  73.2 1.7 copy-done.4
  75.0 9.2 %convolution_convert_fusion.3 = bf16[768,1536]{1,0:T(8,128)(2,1)} fusion(bf16[768,2048]{1,0:T(8,128)(2,1)S(1)} %get-tuple-element.61.activated, bf16[1536,2048]{1,0:T(8,128)(2,1)} %param.26), kind=kOutput, calls=%fused_computation.17 | convolution fusion | flops 4833017856 | bytes 11796480 | tf_op jit(solution)/shard_map/dot_general | solution.py:279
  84.2 0.2 reduce-window.8
  84.4 0.1 select_reduce_fusion.4
  84.5 0.2 select_reduce_fusion.3
  84.7 13.5 %psum.14 = s32[2,12]{1,0:T(2,128)S(1)} all-reduce(s32[2,12]{1,0:T(2,128)S(1)} %pad_add_fusion.1), channel_id=1, replica_groups=mesh['dp'=8,'fsdp'=4] {'dp'}, use_global_device_ids=true, to_apply=%region_12.14 | all-reduce | flops 24 | bytes 192 | tf_op jit(solution)/shard_map/psum | solution.py:248
  98.3 0.1 and.100
  98.4 0.2 select_reduce_fusion.5
  98.7 0.2 reshape.305
  98.9 0.2 reshape.304
  99.1 0.1 copy.60
  99.2 0.1 copy.61
  99.3 0.2 convert_reduce_fusion
  99.6 1.1 gather_fusion.1
  100.7 0.7 fusion.35
  101.5 7.8 %fusion.29 = (f32[192]{0:T(256)S(1)}, f32[192]{0:T(256)S(1)}) fusion(f32[]{:T(128)} %bitcast.18, f32[]{:T(128)} %bitcast.17, f32[]{:T(128)} %bitcast.16, f32[]{:T(128)} %bitcast.15, f32[]{:T(128)} %bitcast.14, f32[]{:T(128)} %bitcast.13, f32[]{:T(128)} %bitcast.12, f32[]{:T(128)} %bitcast.11, f32[]{:T(128)} %bitcast.10, f32[]{:T(128)} %bitcast.9, ...), kind=kLoop, calls=%fused_computation.132 | loop fusion | flops 8832 | bytes 1588 | tf_op jit(solution)/shard_map/mul | solution.py:315
  109.3 10.2 %reduce-scatter.4.cloned.1.call-done = bf16[192,1536]{1,0:T(8,128)(2,1)} async-done(((bf16[768,1536]{1,0:T(8,128)(2,1)}), bf16[192,1536]{1,0:T(8,128)(2,1)}) %reduce-scatter.4.cloned.1.call-update) | async-done | bytes 589840 | tf_op jit(solution)/shard_map/reduce_scatter | solution.py:334
  119.4 1.8 fusion.31
  121.3 0.3 multiply_reduce_fusion.2
  121.5 0.4 multiply_reduce_fusion.3
  121.9 0.1 select_reduce_fusion.1
  122.1 0.6 select_reduce_fusion.8
  122.7 0.7 fusion.34
  123.4 7.5 %select_multiply_fusion = f32[192]{0:T(256)S(1)} fusion(f32[]{:T(128)} %bitcast.36, f32[]{:T(128)} %bitcast.35, f32[]{:T(128)} %bitcast.34, f32[]{:T(128)} %bitcast.33, f32[]{:T(128)} %bitcast.32, f32[]{:T(128)} %bitcast.31, f32[]{:T(128)} %bitcast.30, f32[]{:T(128)} %bitcast.29, f32[]{:T(128)} %bitcast.28, f32[]{:T(128)} %bitcast.27, f32[]{:T(128)} %bitcast.26, ...), kind=kLoop, calls=%fused_computation.95 | loop fusion | flops 8832 | bytes 820 | tf_op jit(solution)/shard_map/mul | solution.py:314
  130.8 0.5 fusion.28
  131.4 1.3 multiply_convert_fusion.1
  132.7 39.9 %psum.15 = f32[]{:T(128)} all-reduce(f32[]{:T(128)} %get-tuple-element.27), channel_id=1, replica_groups=mesh['dp'=8,'fsdp'=4] {'dp','fsdp'}, use_global_device_ids=true, to_apply=%region_19.21 | all-reduce | flops 1 | bytes 8 | tf_op jit(solution)/shard_map/psum | solution.py:351
  173.3 4.5 %copy.54 = bf16[768,1536]{0,1:T(8,128)(2,1)} copy(bf16[768,1536]{1,0:T(8,128)(2,1)} %all-gather.2.cloned.1.call-done) | data formatting | bytes 4718592 | tf_op jit(solution)/shard_map/all_gather | solution.py:355
  177.8 13.0 %fusion.6.dpre = bf16[768,2048]{1,0:T(8,128)(2,1)} fusion(f32[768,2048]{1,0:T(8,128)} %get-tuple-element.62, bf16[768,1536]{1,0:T(8,128)(2,1)S(1)} %copy-done.5, bf16[1536,2048]{1,0:T(8,128)(2,1)} %param.26), kind=kOutput, calls=%fused_computation.13 | convolution fusion | flops 4863295488 | bytes 18087936 | tf_op jit(solution)/shard_map/dot_general | solution.py:356
  190.9 129.5 %gradient_ring.1 = (f32[192,2048]{1,0:T(8,128)}, f32[192,2048]{1,0:T(8,128)}) custom-call(bf16[1536,768]{1,0:T(8,128)(2,1)} %bitcast.78, bf16[768,2048]{1,0:T(8,128)(2,1)} %fusion.6.dpre, bf16[1536,768]{1,0:T(8,128)(2,1)} %bitcast.79, bf16[768,2048]{1,0:T(8,128)(2,1)} %copy-done.4), custom_call_target="tpu_custom_call" | custom-call | tf_op jit(solution)/shard_map/gradient_ring/pallas_call | solution.py:160
  320.4 2.8 copy.71
  323.2 1.1 copy.72
  (71 shorter events, 1.0 us)
Async XLA Ops:
  7.2 20.4 %copy-start = (f32[10,3,1536]{2,1,0:T(4,128)S(1)}, f32[10,3,1536]{2,1,0:T(4,128)}, u32[]{:S(2)}) copy-start(f32[10,3,1536]{2,1,0:T(4,128)} %param.24) | copy-start | bytes 552964
  7.2 5.9 %copy-start.9 = (bf16[12,2,4096]{2,1,0:T(2,128)(2,1)S(1)}, bf16[12,2,4096]{2,1,0:T(2,128)(2,1)}, u32[]{:S(2)}) copy-start(bf16[12,2,4096]{2,1,0:T(2,128)(2,1)} %param.15) | copy-start | bytes 589828
  7.2 112.3 %reduce-scatter.4.cloned.1.call-start = ((), (), s32[]{:S(2)}) async-start(), calls=%async_computation.2 | async-start | bytes 2949120 | tf_op jit(solution)/shard_map/reduce_scatter | solution.py:334
  11.1 8.0 %copy-start.11 = (s32[48]{0:T(128)S(1)}, s32[48]{0:T(128)}, u32[]{:S(2)}) copy-start(s32[48]{0:T(128)} %param.20) | copy-start | bytes 580
  13.9 13.3 %collective-permute-start = (bf16[6,24704]{1,0:T(8,128)(2,1)S(1)}, bf16[6,24704]{1,0:T(8,128)(2,1)S(1)}, u32[]{:S(2)}, u32[]{:S(2)}) collective-permute-start(bf16[6,24704]{1,0:T(8,128)(2,1)S(1)} %slice.110), channel_id=1, source_target_pairs={{0,4},{4,8},{8,12},{12,16},{16,20},{20,24},{24,28},{1,5},{5,9},{9,... | collective-permute-start | bytes 889352 | tf_op jit(solution)/shard_map/ppermute | solution.py:29
  40.2 6.3 %copy-start.8 = (bf16[64,1536]{1,0:T(8,128)(2,1)S(1)}, bf16[64,1536]{1,0:T(8,128)(2,1)}, u32[]{:S(2)}) copy-start(bf16[64,1536]{1,0:T(8,128)(2,1)} %param.23) | copy-start | bytes 589828
  55.5 3.8 %copy-start.2 = (f32[768,1536]{0,1:T(8,128)S(1)}, f32[768,1536]{0,1:T(8,128)}, u32[]{:S(2)}) copy-start(f32[768,1536]{0,1:T(8,128)} %copy.47) | copy-start | bytes 14155780
  55.5 9.1 %slice-start = ((s8[6291456]{0:T(1024)(128)(4,1)}), s8[4194304]{0:T(1024)(128)(4,1)S(1)}, s32[]{:S(2)}) async-start(s8[6291456]{0:T(1024)(128)(4,1)} %bitcast.94), calls=%async_computation.3 | async-start | bytes 8388608
  59.3 5.4 %slice-start.1 = ((s8[6291456]{0:T(1024)(128)(4,1)}), s8[2097152]{0:T(1024)(128)(4,1)S(1)}, s32[]{:S(2)}) async-start(s8[6291456]{0:T(1024)(128)(4,1)} %bitcast.94), calls=%async_computation.4 | async-start | bytes 4194304
  64.7 8.5 %copy-start.3 = (bf16[768,1536]{0,1:T(8,128)(2,1)}, bf16[768,1536]{0,1:T(8,128)(2,1)S(1)}, u32[]{:S(2)}) copy-start(bf16[768,1536]{0,1:T(8,128)(2,1)S(1)} %add_convert_fusion) | copy-start | bytes 7077892
  73.2 1.8 copy-start.4
  75.0 9.3 %copy-start.12 = (s32[12]{0:T(128)S(1)}, s32[12]{0:T(128)}, u32[]{:S(2)}) copy-start(s32[12]{0:T(128)} %param.22) | copy-start | bytes 148
  75.0 9.5 %copy-start.10 = (s32[48]{0:T(128)S(1)}, s32[48]{0:T(128)}, u32[]{:S(2)}) copy-start(s32[48]{0:T(128)} %param.21) | copy-start | bytes 580
  75.0 9.5 %copy-start.13 = (s32[12]{0:T(128)S(1)}, s32[12]{0:T(128)}, u32[]{:S(2)}) copy-start(s32[12]{0:T(128)} %param.19) | copy-start | bytes 148
  84.2 89.1 %all-gather.2.cloned.1.call-start = ((), (), s32[]{:S(2)}) async-start(), calls=%async_computation.1 | async-start | bytes 2949120 | tf_op jit(solution)/shard_map/all_gather | solution.py:355
  100.7 20.8 %copy-start.7 = (bf16[1536,64]{0,1:T(8,128)(2,1)S(1)}, bf16[1536,64]{0,1:T(8,128)(2,1)}, u32[]{:S(2)}) copy-start(bf16[1536,64]{0,1:T(8,128)(2,1)} %param.27) | copy-start | bytes 589828
  173.3 4.5 %copy-start.5 = (bf16[768,1536]{1,0:T(8,128)(2,1)S(1)}, bf16[768,1536]{1,0:T(8,128)(2,1)}, u32[]{:S(2)}) copy-start(bf16[768,1536]{1,0:T(8,128)(2,1)} %all-gather.2.cloned.1.call-done) | copy-start | bytes 7077892
  320.4 2.9 copy-start.6
  320.4 4.0 %copy-start.1 = (f32[10,3,1536]{2,1,0:T(4,128)S(1)}, f32[10,3,1536]{2,1,0:T(4,128)}, u32[]{:S(2)}) copy-start(f32[10,3,1536]{2,1,0:T(4,128)} %param.24) | copy-start | bytes 552964
Sparse Core Ops, SparseCore 0:
  84.3 35.0 reduce-scatter.3
  132.9 24.2 all-gather.1

commit v2 on v1

--- a/solution.py
+++ b/solution.py
@@ -78,18 +78,87 @@
 
 
 def gradient_ring(
-    count, pieces, modulated, dpre, upstream, activated, up_out, down_out, sent, came, send_sem, recv_sem
+    count,
+    pieces,
+    modulated_rows,
+    dpre,
+    upstream_rows,
+    activated,
+    loss,
+    up_out,
+    down_out,
+    loss_out,
+    modulated,
+    upstream,
+    sent,
+    came,
+    loss_mid,
+    loss_fsdp,
+    loss_dp,
+    send_sem,
+    recv_sem,
+    fsdp_send,
+    fsdp_recv,
+    dp_send,
+    dp_recv,
 ):
     index = lax.axis_index("dp")
+    column = lax.axis_index("fsdp")
+    columns = lax.axis_size("fsdp")
     place = ring_place(index, count)
     following = ring_index((place + 1) % count, count)
     preceding = ring_index((place + count - 1) % count, count)
     barrier = pltpu.get_barrier_semaphore()
-    for neighbour in (following, preceding):
-        pl.semaphore_signal(
-            barrier, inc=1, device_id={"dp": neighbour}, device_id_type=pl.DeviceIdType.MESH
-        )
-    pl.semaphore_wait(barrier, 2)
+
+    def greet(axis, member, size):
+        def one(ahead, carry):
+            pl.semaphore_signal(
+                barrier,
+                inc=1,
+                device_id={axis: (member + ahead) % size},
+                device_id_type=pl.DeviceIdType.MESH,
+            )
+            return carry
+
+        lax.fori_loop(1, size, one, 0)
+
+    greet("dp", index, count)
+    greet("fsdp", column, columns)
+    for rows_ref, turned in ((upstream_rows, upstream), (modulated_rows, modulated)):
+        for start in range(0, turned.shape[0], 256):
+            turned[start : start + 256, :] = rows_ref[:, start : start + 256].T
+    pl.semaphore_wait(barrier, count - 1 + columns - 1)
+
+    def loss_copy(axis, member, size, source, slots, send, recv, ahead):
+        return pltpu.make_async_remote_copy(
+            src_ref=source,
+            dst_ref=slots.at[ahead - 1],
+            send_sem=send.at[ahead - 1],
+            recv_sem=recv.at[ahead - 1],
+            device_id={axis: (member + ahead) % size},
+            device_id_type=pl.DeviceIdType.MESH,
+        )
+
+    fsdp_copy = functools.partial(
+        loss_copy, "fsdp", column, columns, loss, loss_fsdp, fsdp_send, fsdp_recv
+    )
+    dp_copy = functools.partial(loss_copy, "dp", index, count, loss_mid, loss_dp, dp_send, dp_recv)
+
+    def start_all(make, size):
+        def one(ahead, carry):
+            make(ahead).start()
+            return carry
+
+        lax.fori_loop(1, size, one, 0)
+
+    def collect(make, size, first, slots):
+        def one(ahead, total):
+            make(ahead).wait()
+            return total + slots[ahead - 1]
+
+        return lax.fori_loop(1, size, one, first)
+
+    start_all(fsdp_copy, columns)
     block = modulated.shape[0] // count
     span = dpre.shape[1] // pieces
     factors = ((modulated, dpre), (upstream, activated))
@@ -134,6 +203,8 @@
             copy(way, step, piece).start()
         return carry
 
+    loss_mid[...] = collect(fsdp_copy, columns, loss[...], loss_fsdp)
+    start_all(dp_copy, count)
     lax.fori_loop(1, count - 1, hop, 0)
     for way, piece in order:
         part = own(way, count - 1, piece)
@@ -148,31 +219,195 @@
         return carry
 
     lax.fori_loop(0, count - 1, drain, 0)
-
-
-def reduced_gradients(modulated, dpre, upstream, activated):
+    loss_out[...] = collect(dp_copy, count, loss_mid[...], loss_dp)
+
+
+def reduced_gradients(modulated, dpre, upstream, activated, loss):
     count = lax.axis_size("dp")
+    columns = lax.axis_size("fsdp")
     pieces = max(1, 32 // count)
-    block = modulated.shape[0] // count
+    rows, width = modulated.shape
+    block = width // count
+    tile = (8, 128)
     span = dpre.shape[1] // pieces
     shape = jax.ShapeDtypeStruct((block, dpre.shape[1]), jnp.float32)
     hops = (2, pieces, count - 1)
     return pl.pallas_call(
         functools.partial(gradient_ring, count, pieces),
-        out_shape=(shape, shape),
-        in_specs=[pl.BlockSpec(memory_space=pltpu.VMEM)] * 4,
-        out_specs=(pl.BlockSpec(memory_space=pltpu.VMEM),) * 2,
+        out_shape=(shape, shape, jax.ShapeDtypeStruct(tile, jnp.float32)),
+        in_specs=[pl.BlockSpec(memory_space=pltpu.VMEM)] * 5,
+        out_specs=(pl.BlockSpec(memory_space=pltpu.VMEM),) * 3,
         scratch_shapes=[
+            pltpu.VMEM((width, rows), jnp.bfloat16),
+            pltpu.VMEM((width, rows), jnp.bfloat16),
             pltpu.VMEM(hops + (block, span), jnp.bfloat16),
             pltpu.VMEM(hops + (block, span), jnp.bfloat16),
+            pltpu.VMEM(tile, jnp.float32),
+            pltpu.VMEM((columns - 1,) + tile, jnp.float32),
+            pltpu.VMEM((count - 1,) + tile, jnp.float32),
             pltpu.SemaphoreType.DMA(hops),
             pltpu.SemaphoreType.DMA(hops),
+            pltpu.SemaphoreType.DMA((columns - 1,)),
+            pltpu.SemaphoreType.DMA((columns - 1,)),
+            pltpu.SemaphoreType.DMA((count - 1,)),
+            pltpu.SemaphoreType.DMA((count - 1,)),
         ],
         compiler_params=pltpu.CompilerParams(
             collective_id=0, has_side_effects=True, vmem_limit_bytes=56 * 1024 * 1024
         ),
         name="gradient_ring",
-    )(modulated, dpre, upstream, activated)
+    )(modulated, dpre, upstream, activated, jnp.broadcast_to(loss, tile))
+
+
+def pair_copy(source, target, send, recv, member):
+    return pltpu.make_async_remote_copy(
+        src_ref=source,
+        dst_ref=target,
+        send_sem=send,
+        recv_sem=recv,
+        device_id={"fsdp": member},
+        device_id_type=pl.DeviceIdType.MESH,
+    )
+
+
+def pair_barrier(half, line, core):
+    barrier = pltpu.get_barrier_semaphore()
+    others = [2 * ((line + ahead) % half) + core for ahead in range(1, half)]
+    for member in [2 * line + 1 - core] + others:
+        pl.semaphore_signal(
+            barrier, inc=1, device_id={"fsdp": member}, device_id_type=pl.DeviceIdType.MESH
+        )
+    pl.semaphore_wait(barrier, half)
+
+
+def scatter_kernel(half, values, out, paired, merged, came, send_a, recv_a, send_b, recv_b):
+    member = lax.axis_index("fsdp")
+    line, core = member // 2, member % 2
+    pair_barrier(half, line, core)
+
+    def to_pair(ahead):
+        return pair_copy(
+            values.at[2 * ((line + ahead) % half) + 1 - core],
+            paired.at[ahead],
+            send_a.at[ahead],
+            recv_a.at[ahead],
+            2 * line + 1 - core,
+        )
+
+    def to_line(ahead):
+        return pair_copy(
+            merged.at[ahead - 1],
+            came.at[ahead - 1],
+            send_b.at[ahead - 1],
+            recv_b.at[ahead - 1],
+            2 * ((line + ahead) % half) + core,
+        )
+
+    order = list(range(1, half)) + [0]
+    for ahead in order:
+        to_pair(ahead).start()
+    for ahead in order:
+        to_pair(ahead).wait_recv()
+        both = values[2 * ((line + ahead) % half) + core].astype(jnp.float32) + paired[
+            ahead
+        ].astype(jnp.float32)
+        if ahead:
+            merged[ahead - 1] = both.astype(jnp.bfloat16)
+            to_line(ahead).start()
+        else:
+            out[...] = both
+    for ahead in range(1, half):
+        to_line(ahead).wait_recv()
+        out[...] += came[ahead - 1].astype(jnp.float32)
+    for ahead in order:
+        to_pair(ahead).wait_send()
+        if ahead:
+            to_line(ahead).wait_send()
+
+
+def scattered_sums(values):
+    members = lax.axis_size("fsdp")
+    half = members // 2
+    share = (values.shape[0] // members, values.shape[1])
+    vmem = pl.BlockSpec(memory_space=pltpu.VMEM)
+    return pl.pallas_call(
+        functools.partial(scatter_kernel, half),
+        out_shape=jax.ShapeDtypeStruct(share, jnp.float32),
+        in_specs=[vmem],
+        out_specs=vmem,
+        scratch_shapes=[
+            pltpu.VMEM((half,) + share, jnp.bfloat16),
+            pltpu.VMEM((half - 1,) + share, jnp.bfloat16),
+            pltpu.VMEM((half - 1,) + share, jnp.bfloat16),
+            pltpu.SemaphoreType.DMA((half,)),
+            pltpu.SemaphoreType.DMA((half,)),
+            pltpu.SemaphoreType.DMA((half - 1,)),
+            pltpu.SemaphoreType.DMA((half - 1,)),
+        ],
+        compiler_params=pltpu.CompilerParams(
+            collective_id=1, has_side_effects=True, vmem_limit_bytes=32 * 1024 * 1024
+        ),
+        name="pair_scatter",
+    )(values.reshape((members,) + share))
+
+
+def gather_kernel(half, value, out, send_a, recv_a, send_b, recv_b):
+    member = lax.axis_index("fsdp")
+    line, core = member // 2, member % 2
+    pair_barrier(half, line, core)
+
+    def to_pair(ahead):
+        slot = 2 * ((line + half - ahead) % half) + core
+        return pair_copy(
+            out.at[slot] if ahead else value,
+            out.at[slot],
+            send_a.at[ahead],
+            recv_a.at[ahead],
+            2 * line + 1 - core,
+        )
+
+    def to_line(ahead):
+        return pair_copy(
+            value,
+            out.at[member],
+            send_b.at[ahead - 1],
+            recv_b.at[ahead - 1],
+            2 * ((line + ahead) % half) + core,
+        )
+
+    for ahead in range(1, half):
+        to_line(ahead).start()
+    to_pair(0).start()
+    out[member] = value[...]
+    for ahead in range(1, half):
+        to_line(ahead).wait_recv()
+        to_pair(ahead).start()
+    for ahead in range(half):
+        to_pair(ahead).wait()
+        if ahead:
+            to_line(ahead).wait_send()
+
+
+def gathered_rows(value):
+    members = lax.axis_size("fsdp")
+    half = members // 2
+    vmem = pl.BlockSpec(memory_space=pltpu.VMEM)
+    return pl.pallas_call(
+        functools.partial(gather_kernel, half),
+        out_shape=jax.ShapeDtypeStruct((members,) + value.shape, value.dtype),
+        in_specs=[vmem],
+        out_specs=vmem,
+        scratch_shapes=[
+            pltpu.SemaphoreType.DMA((half,)),
+            pltpu.SemaphoreType.DMA((half,)),
+            pltpu.SemaphoreType.DMA((half - 1,)),
+            pltpu.SemaphoreType.DMA((half - 1,)),
+        ],
+        compiler_params=pltpu.CompilerParams(
+            collective_id=2, has_side_effects=True, vmem_limit_bytes=32 * 1024 * 1024
+        ),
+        name="pair_gather",
+    )(value).reshape(members * value.shape[0], value.shape[1])
 
 
 def shards(
@@ -292,6 +527,9 @@
     def head_terms(summed, lower, count):
         row_ids = lower + jnp.arange(count, dtype=jnp.int32)
         owner_unit = row_ids // seq
+        unit_member = (owner_unit[:, None] == jnp.arange(units, dtype=jnp.int32)[None, :]).astype(
+            jnp.float32
+        )
         gate_rows = jnp.take(gates, owner_unit, axis=0)
         mixed = lax.dynamic_slice_in_dim(embedded_rows, lower, count) + gate_rows * summed
         final, inverse = layer_norm(mixed)
@@ -300,16 +538,13 @@
         )
         target = lax.dynamic_slice_in_dim(old_rows, lower, count).astype(jnp.float32)
         drawn = lax.dynamic_slice_in_dim(noise_rows, lower, count).astype(jnp.float32)
-        coeff_rows = jnp.take(coeff, owner_unit)[:, None]
+        coeff_rows = jnp.sum(unit_member * coeff[None, :], axis=1, keepdims=True)
         error = velocity - target
         terms = coeff_rows * drawn * error + 0.5 * coeff_rows * coeff_rows * error * error
-        unit_member = (owner_unit[:, None] == jnp.arange(units, dtype=jnp.int32)[None, :]).astype(
-            jnp.float32
-        )
         unit_sums = jnp.sum(unit_member * jnp.sum(terms, axis=1)[:, None], axis=0)
 
         def backward(loss_slope):
-            slope_rows = jnp.take(loss_slope, owner_unit)[:, None]
+            slope_rows = jnp.sum(unit_member * loss_slope[None, :], axis=1, keepdims=True)
             dvelocity = (
                 slope_rows
                 * (-(coeff_rows * drawn + coeff_rows * coeff_rows * error) / (seq * patch))
@@ -331,9 +566,7 @@
 
     share = rows // lax.axis_size("fsdp")
     lower = lax.axis_index("fsdp") * share
-    summed = lax.psum_scatter(
-        projected, "fsdp", scatter_dimension=0, tiled=True
-    ).astype(jnp.float32)
+    summed = scattered_sums(projected)
     part_sums, backward = head_terms(summed, lower, share)
     whole_units = share % seq == 0
     unit_sums = part_sums if whole_units else lax.psum(part_sums, "fsdp")
@@ -348,16 +581,17 @@
     if whole_units:
         unit_ids = jnp.arange(units, dtype=jnp.int32)
         mine = (unit_ids >= lower // seq) & (unit_ids < (lower + share) // seq)
-        total_count = lax.psum(jnp.sum(jnp.where(mine, unit_loss, 0.0)), ("dp", "fsdp"))
     else:
-        total_count = lax.psum(jnp.sum(unit_loss), "dp")
-    total_count = total_count / (surviving_count * step_indices)
-    upstream = lax.all_gather(backward(loss_slope), "fsdp", axis=0, tiled=True)
+        mine = jnp.full((units,), lower == 0)
+    loss_part = jnp.sum(jnp.where(mine, unit_loss, 0.0))
+    upstream = gathered_rows(backward(loss_slope))
     dactivated = jnp.dot(upstream, down_projection_weight, preferred_element_type=jnp.float32)
     unused_value, pull = jax.vjp(smooth_gate, pre)
     dpre = pull(dactivated)[0].astype(jnp.bfloat16)
-    up_gradient, down_gradient = reduced_gradients(modulated.T, dpre, upstream.T, activated)
-    return (up_gradient, down_gradient, total_count)
+    up_gradient, down_gradient, loss_sum = reduced_gradients(
+        modulated, dpre, upstream, activated, loss_part
+    )
+    return (up_gradient, down_gradient, loss_sum[0, 0] / (surviving_count * step_indices))
 
 
 def solution(mesh):

time: 333 us -> 245 us (0.74)
  blocking collectives: 53.4 us -> 11.9 us
  Pallas kernels: 130 us -> 170 us
  local copies, waits for them, and re-layouts: 42.9 us -> 16.4 us
  other arithmetic: 31.2 us -> 8.63 us
  waiting for transfers between devices: 18.3 us -> 0.01 us
  between operations: 16.3 us -> 2.96 us
  matrix products: 35.5 us -> 29.7 us
    psum x1 -> x0, blocking collectives: 39.9 us -> none  [shards(): lax.psum(jnp.sum(jnp.where(mine, unit_loss, 0.0)), ('dp', 'fsdp'))]
    pallas_call x0 -> x2, Pallas kernels: none -> 34.8 us  [the longest x1 17.9 us: scattered_sums(): pl.pallas_call(functools.partial(scatter_kernel, half), out_shape=jax.Sha...]
    reduce_scatter x1 -> x0, waiting for transfers between devices: 10.2 us -> none  [shards(): lax.psum_scatter(projected, 'fsdp', scatter_dimension=0, tiled=True)]
    mul x2 -> x0, local copies, waits for them, and re-layouts: 8.83 us -> none  [shards(): normed * (1.0 + modulation[:, 1][:, None]) + modulation[:, 0][:, None]]
    add x2 -> x0, local copies, waits for them, and re-layouts: 8.79 us -> none  [shards(): normed * (1.0 + modulation[:, 1][:, None]) + modulation[:, 0][:, None]]
    ppermute x1, waiting for transfers between devices: 8.1 us -> 0.01 us  [shifted(): lax.ppermute(value, axis, [(source, source + steps) for source in range(i...]
    mul x1 -> x0, other arithmetic: 7.8 us -> none  [backward(): coeff_rows * coeff_rows * error]
    mul x1, other arithmetic: 7.45 us -> 0.01 us  [backward(): slope_rows * (-(coeff_rows * drawn + coeff_rows * coeff_rows * error) / (...]
  transfers between devices with their start and end apart: 3 -> 1, of which waited for: 2 -> 0; matrix products, arithmetic and copies ran while one was open for 3% -> 0% of each run, Pallas kernels for 0% -> 0%
where the time goes in v2:
time: 245 us; the launch traced here: 244 us
  Pallas kernels  170 us (69%)
  matrix products  29.7 us (12%)
  local copies, waits for them, and re-layouts  16.4 us (7%)
  blocking collectives  11.9 us (5%)
  other arithmetic  8.63 us (4%)
  starting transfers between devices  4.89 us (2%)
  between operations  2.96 us (1%)
    pallas_call x1, Pallas kernels, reduced_gradients(): pl.pallas_call(functools.partial(gradient_ring, count, pieces), out_shape...  135 us
    pallas_call x1, Pallas kernels, scattered_sums(): pl.pallas_call(functools.partial(scatter_kernel, half), out_shape=jax.Sha...  17.9 us
    pallas_call x1, Pallas kernels, gathered_rows(): pl.pallas_call(functools.partial(gather_kernel, half), out_shape=jax.Shap...  16.9 us
    dot_general x1, matrix products, shards(): jnp.dot(upstream, down_projection_weight, preferred_element_type=jnp.floa...  13.8 us
    psum x1, blocking collectives, shards(): totals = lax.psum(partial_value, 'dp')  11.9 us
    unnamed x48, local copies, waits for them, and re-layouts  9.2 us
    dot_general x1, matrix products, shards(): jnp.dot(modulated, up_projection_weight, preferred_element_type=jnp.float32)  7.92 us
    dot_general x1, matrix products, shards(): lax.dot_general(activated, down_projection_weight, (((1,), (1,)), ((), ()...  5.34 us
  transfers between devices with their start and end apart: 1, of which 0 were waited for; matrix products, arithmetic and copies ran while one was open for 0% of the time, Pallas kernels for 0%

profile of v2, /device:TPU:0, one launch (start us, length us, event | category | flops | bytes accessed | tf_op | source)
XLA Modules:
  0.0 244.2 jit_solution(12903729888583948847)
XLA Ops:
  0.7 0.7 fusion.28
  1.4 0.8 fusion.34
  2.2 0.1 pad_add_fusion.2
  2.3 0.1 iota_compare_fusion.5
  2.4 0.7 pad_add_fusion
  3.1 0.3 select_reduce_fusion
  3.4 1.1 pad.22
  4.5 0.2 copy.31
  4.7 0.3 convolution_convert_fusion
  5.0 1.1 pad.21
  6.1 0.2 copy.30
  6.3 0.3 convolution_convert_fusion.1
  6.6 0.2 pad.20
  6.8 0.2 copy.29
  6.9 0.3 convolution_convert_fusion.2
  7.2 0.1 fusion.10
  7.3 0.1 slice.64
  7.4 4.9 %collective-permute-start = (bf16[6,24704]{1,0:T(8,128)(2,1)S(1)}, bf16[6,24704]{1,0:T(8,128)(2,1)S(1)}, u32[]{:S(2)}, u32[]{:S(2)}) collective-permute-start(bf16[6,24704]{1,0:T(8,128)(2,1)S(1)} %slice.64), channel_id=1, source_target_pairs={{0,4},{4,8},{8,12},{12,16},{16,20},{20,24},{24,28},{1,5},{5,9},{9,... | collective-permute-start | bytes 889352 | tf_op jit(solution)/shard_map/ppermute | solution.py:29
  12.4 0.1 select_reduce_fusion.6
  12.5 0.1 dynamic-slice_compare_fusion
  12.6 0.2 reduce-window.8
  12.8 0.2 select_reduce_fusion.5
  13.0 0.1 and.96
  13.1 11.9 %psum.7 = s32[2,12]{1,0:T(2,128)S(1)} all-reduce(s32[2,12]{1,0:T(2,128)S(1)} %pad_add_fusion.1), channel_id=1, replica_groups=mesh['dp'=8,'fsdp'=4] {'dp'}, use_global_device_ids=true, to_apply=%region_12.13 | all-reduce | flops 24 | bytes 192 | tf_op jit(solution)/shard_map/psum | solution.py:483
  25.0 0.2 select_reduce_fusion.7
  25.3 0.1 slice_select_fusion
  25.5 0.1 reshape.346
  25.5 0.1 reshape.345
  25.6 0.2 convert_reduce_fusion
  25.8 0.2 reshape.344
  26.1 0.7 gather_fusion
  26.8 0.1 broadcast_select_fusion
  26.9 0.2 fusion.33
  27.1 0.8 fusion.35
  28.0 0.6 multiply_reduce_fusion
  28.6 0.9 fusion.7.modulated_rows
  29.6 0.8 copy-done.2
  30.4 1.3 slice-done.1
  31.7 7.9 %multiply_convert_fusion = (bf16[768,2048]{1,0:T(8,128)(2,1)S(1)}, f32[768,2048]{1,0:T(8,128)}) fusion(bf16[768,1536]{1,0:T(8,128)(2,1)S(1)} %fusion.7.modulated_rows, bf16[1536,2048]{1,0:T(8,128)(2,1)S(1)} %bitcast.76), kind=kOutput, calls=%fused_computation.14 | convolution fusion | flops 4845993984 | bytes 18087936 | tf_op jit(solution)/shard_map/dot_general | solution.py:512
  39.6 5.3 %convolution_convert_fusion.3 = bf16[768,1536]{1,0:T(8,128)(2,1)S(1)} fusion(bf16[768,2048]{1,0:T(8,128)(2,1)S(1)} %get-tuple-element.38.activated, bf16[1536,2048]{1,0:T(8,128)(2,1)S(1)} %bitcast.78), kind=kOutput, calls=%fused_computation.19 | convolution fusion | flops 4833017856 | bytes 11796480 | tf_op jit(solution)/shard_map/dot_general | solution.py:514
  45.0 17.9 %pair_scatter.1 = f32[192,1536]{1,0:T(8,128)S(1)} custom-call(bf16[4,192,1536]{2,1,0:T(8,128)(2,1)S(1)} %bitcast.59), custom_call_target="tpu_custom_call" | custom-call | tf_op jit(solution)/shard_map/pair_scatter/pallas_call | solution.py:333
  62.8 2.0 gather_fusion.1
  64.9 2.0 fusion.31
  66.9 0.3 multiply_reduce_fusion.2
  67.2 0.2 reshape.349
  67.4 0.2 reshape.348
  67.6 0.1 copy.27
  67.7 0.1 select_reduce_fusion.3
  67.8 0.1 copy.28
  67.9 0.1 broadcast_in_dim.76
  68.0 0.1 reshape.352
  68.0 0.4 multiply_reduce_fusion.3
  68.4 0.1 select_reduce_fusion.2
  68.6 0.6 select_reduce_fusion.10
  69.2 0.1 select_reduce_fusion.1
  69.3 0.5 fusion.29
  69.8 0.5 multiply_convert_fusion.1.value
  70.3 16.9 %pair_gather.1 = bf16[4,192,1536]{2,1,0:T(8,128)(2,1)S(1)} custom-call(bf16[192,1536]{1,0:T(8,128)(2,1)S(1)} %multiply_convert_fusion.1.value), custom_call_target="tpu_custom_call" | custom-call | tf_op jit(solution)/shard_map/pair_gather/pallas_call | solution.py:395
  87.2 13.8 %fusion.6.dpre = bf16[768,2048]{1,0:T(8,128)(2,1)} fusion(f32[768,2048]{1,0:T(8,128)} %get-tuple-element.39, bf16[768,1536]{1,0:T(8,128)(2,1)S(1)} %bitcast.57, bf16[1536,2048]{1,0:T(8,128)(2,1)} %param.24), kind=kOutput, calls=%fused_computation.13 | convolution fusion | flops 4863295488 | bytes 18087936 | tf_op jit(solution)/shard_map/dot_general | solution.py:588
  101.1 1.2 broadcast_in_dim.77.loss
  102.3 134.9 %gradient_ring.1 = (f32[192,2048]{1,0:T(8,128)}, f32[192,2048]{1,0:T(8,128)}, f32[8,128]{1,0:T(8,128)}) custom-call(bf16[768,1536]{1,0:T(8,128)(2,1)} %copy-done.4, bf16[768,2048]{1,0:T(8,128)(2,1)} %fusion.6.dpre, bf16[768,1536]{1,0:T(8,128)(2,1)} %bitcast.58, bf16[768,2048]{1,0:T(8,128)(2,1)} %copy-done.5, f32[8,128]{1,0:T(8,128)} %broadcast_in_dim.77.loss), custom_call_target="tpu_custom_call" | custom-call | tf_op jit(solution)/shard_map/gradient_ring/pallas_call | solution.py:235
  237.2 1.3 slice.59
  239.2 2.7 %copy.38 = f32[192,2048]{1,0:T(8,128)} copy(f32[192,2048]{1,0:T(8,128)} %get-tuple-element.50) | data formatting | bytes 3145728
  241.9 1.1 copy.39
  (66 shorter events, 0.4 us)
Async XLA Ops:
  0.6 25.4 %copy-start = (f32[10,3,1536]{2,1,0:T(4,128)S(1)}, f32[10,3,1536]{2,1,0:T(4,128)}, u32[]{:S(2)}) copy-start(f32[10,3,1536]{2,1,0:T(4,128)} %param.22) | copy-start | bytes 552964
  0.6 5.9 %copy-start.9 = (bf16[12,2,4096]{2,1,0:T(2,128)(2,1)S(1)}, bf16[12,2,4096]{2,1,0:T(2,128)(2,1)}, u32[]{:S(2)}) copy-start(bf16[12,2,4096]{2,1,0:T(2,128)(2,1)} %param.13) | copy-start | bytes 589828
  4.5 7.9 %copy-start.10 = (s32[48]{0:T(128)S(1)}, s32[48]{0:T(128)}, u32[]{:S(2)}) copy-start(s32[48]{0:T(128)} %param.19) | copy-start | bytes 580
  4.5 7.9 %copy-start.13 = (s32[12]{0:T(128)S(1)}, s32[12]{0:T(128)}, u32[]{:S(2)}) copy-start(s32[12]{0:T(128)} %param.17) | copy-start | bytes 148
  4.5 8.0 %copy-start.11 = (s32[48]{0:T(128)S(1)}, s32[48]{0:T(128)}, u32[]{:S(2)}) copy-start(s32[48]{0:T(128)} %param.18) | copy-start | bytes 580
  4.5 8.1 %copy-start.12 = (s32[12]{0:T(128)S(1)}, s32[12]{0:T(128)}, u32[]{:S(2)}) copy-start(s32[12]{0:T(128)} %param.20) | copy-start | bytes 148
  7.2 19.9 %copy-start.8 = (bf16[64,1536]{1,0:T(8,128)(2,1)S(1)}, bf16[64,1536]{1,0:T(8,128)(2,1)}, u32[]{:S(2)}) copy-start(bf16[64,1536]{1,0:T(8,128)(2,1)} %param.21) | copy-start | bytes 589828
  7.4 17.8 %collective-permute-start = (bf16[6,24704]{1,0:T(8,128)(2,1)S(1)}, bf16[6,24704]{1,0:T(8,128)(2,1)S(1)}, u32[]{:S(2)}, u32[]{:S(2)}) collective-permute-start(bf16[6,24704]{1,0:T(8,128)(2,1)S(1)} %slice.64), channel_id=1, source_target_pairs={{0,4},{4,8},{8,12},{12,16},{16,20},{20,24},{24,28},{1,5},{5,9},{9,... | collective-permute-start | bytes 889352 | tf_op jit(solution)/shard_map/ppermute | solution.py:29
  27.1 3.2 %slice-start = ((s8[6291456]{0:T(1024)(128)(4,1)}), s8[4194304]{0:T(1024)(128)(4,1)S(1)}, s32[]{:S(2)}) async-start(s8[6291456]{0:T(1024)(128)(4,1)} %bitcast.75), calls=%async_computation | async-start | bytes 8388608
  28.0 2.4 copy-start.2
  28.0 3.7 %slice-start.1 = ((s8[6291456]{0:T(1024)(128)(4,1)}), s8[2097152]{0:T(1024)(128)(4,1)S(1)}, s32[]{:S(2)}) async-start(s8[6291456]{0:T(1024)(128)(4,1)} %bitcast.75), calls=%async_computation.1 | async-start | bytes 4194304
  28.6 11.0 %slice-start.2 = ((s8[6291456]{0:T(1024)(128)(4,1)}), s8[4194304]{0:T(1024)(128)(4,1)S(1)}, s32[]{:S(2)}) async-start(s8[6291456]{0:T(1024)(128)(4,1)} %bitcast.77), calls=%async_computation.2 | async-start | bytes 8388608
  31.7 7.9 %copy-start.4 = (bf16[768,1536]{1,0:T(8,128)(2,1)}, bf16[768,1536]{1,0:T(8,128)(2,1)S(1)}, u32[]{:S(2)}) copy-start(bf16[768,1536]{1,0:T(8,128)(2,1)S(1)} %fusion.7.modulated_rows) | copy-start | bytes 7077892
  31.7 7.9 %slice-start.3 = ((s8[6291456]{0:T(1024)(128)(4,1)}), s8[2097152]{0:T(1024)(128)(4,1)S(1)}, s32[]{:S(2)}) async-start(s8[6291456]{0:T(1024)(128)(4,1)} %bitcast.77), calls=%async_computation.3 | async-start | bytes 4194304
  39.6 5.4 %copy-start.5 = (bf16[768,2048]{1,0:T(8,128)(2,1)}, bf16[768,2048]{1,0:T(8,128)(2,1)S(1)}, u32[]{:S(2)}) copy-start(bf16[768,2048]{1,0:T(8,128)(2,1)S(1)} %get-tuple-element.38.activated) | copy-start | bytes 9437188
  64.9 3.1 %copy-start.7 = (bf16[1536,64]{0,1:T(8,128)(2,1)S(1)}, bf16[1536,64]{0,1:T(8,128)(2,1)}, u32[]{:S(2)}) copy-start(bf16[1536,64]{0,1:T(8,128)(2,1)} %param.25) | copy-start | bytes 589828
  66.9 3.0 %copy-start.3 = (f32[192,1536]{1,0:T(8,128)S(1)}, f32[192,1536]{1,0:T(8,128)}, u32[]{:S(2)}) copy-start(f32[192,1536]{1,0:T(8,128)} %gather_fusion.1) | copy-start | bytes 3538948
  87.2 13.8 %copy-start.1 = (bf16[4,192,1536]{2,1,0:T(8,128)(2,1)}, bf16[4,192,1536]{2,1,0:T(8,128)(2,1)S(1)}, u32[]{:S(2)}) copy-start(bf16[4,192,1536]{2,1,0:T(8,128)(2,1)S(1)} %pair_gather.1) | copy-start | bytes 7077892
  237.2 4.7 %copy-start.6 = (f32[192,2048]{1,0:T(8,128)S(1)}, f32[192,2048]{1,0:T(8,128)}, u32[]{:S(2)}) copy-start(f32[192,2048]{1,0:T(8,128)} %get-tuple-element.51) | copy-start | bytes 4718596
